TPU v7x, 512 devices: a whole 4x4x16 slice. The times are simulated.
512 devices in a mesh: shift: 8 (over x, core), batch: 16 (over z), cols: 4 (over y).
Axes of the slice: x: 4, y: 4, z: 16, core: 2. Of those that a mesh axis runs over, the one named last changes fastest.
Arguments:
- partial_up: float32 [128, 768, 3072], P(('shift', 'batch'), None, 'cols'), parts along dimension 0, may hold values from -0.875 to 0.875
- partial_down: float32 [128, 3072, 768], P(('shift', 'batch'), 'cols'), parts along dimension 0, may hold values from -0.875 to 0.875
- partial_norm: float32 [128, 768], P(('shift', 'batch')), parts along dimension 0, may hold values from -8 to 8
- partial_bias: float32 [128, 768], P(('shift', 'batch')), parts along dimension 0, may hold values from -8 to 8
- master_up: float32 [6144, 3072], P(('shift', 'batch'), 'cols'), parts along dimension 0, may hold values from -0.21875 to 0.21875
- master_down: float32 [24576, 768], P(('shift', 'cols'), 'batch'), parts along dimension 0, may hold values from -0.109375 to 0.109375
- master_norm: float32 [6144], P(('shift', 'batch')), parts along dimension 0, may hold values from 0.25 to 1.75
- master_bias: float32 [6144], P(('shift', 'batch')), parts along dimension 0, may hold values from -3 to 3
- memory_up: float32 [6144, 3072], P(('shift', 'batch'), 'cols'), parts along dimension 0, may hold values from -1.75 to 1.75
- memory_down: float32 [24576, 768], P(('shift', 'cols'), 'batch'), parts along dimension 0, may hold values from -1.75 to 1.75
- memory_norm: float32 [6144], P(('shift', 'batch')), parts along dimension 0, may hold values from -1.75 to 1.75
- memory_bias: float32 [6144], P(('shift', 'batch')), parts along dimension 0, may hold values from -1.75 to 1.75
Outputs:
- compute_up: bfloat16 [6144, 3072], P('shift', 'cols'), parts along dimension 0
- compute_down: bfloat16 [24576, 768], P(('shift', 'cols')), parts along dimension 0
- compute_norm: bfloat16 [6144], P('shift'), parts along dimension 0
- compute_bias: bfloat16 [6144], P('shift'), parts along dimension 0
- stepped_up: float32 [6144, 3072], P(('shift', 'batch'), 'cols'), parts along dimension 0
- stepped_down: float32 [24576, 768], P(('shift', 'cols'), 'batch'), parts along dimension 0
- stepped_norm: float32 [6144], P(('shift', 'batch')), parts along dimension 0
- stepped_bias: float32 [6144], P(('shift', 'batch')), parts along dimension 0
- state_new_up: float32 [6144, 3072], P(('shift', 'batch'), 'cols'), parts along dimension 0
- state_new_down: float32 [24576, 768], P(('shift', 'cols'), 'batch'), parts along dimension 0
- state_new_norm: float32 [6144], P(('shift', 'batch')), parts along dimension 0
- state_new_bias: float32 [6144], P(('shift', 'batch')), parts along dimension 0
There are 8 independent parts, one for each index of `shift`. A program takes and returns all parts, laid end to end along the dimension named above; each array names one. Nothing has to cross between parts.
All inputs are finite; a program needn't handle non-finite values.
Results may differ from a plain program's by a relative error of at most 0.0085.
Values may be sent and summed in bfloat16 or wider, within the bound.
No kernel may reach another device: no remote copies, remote signals or barrier semaphores. Data moves between devices by JAX's collectives and lax.ppermute only.
A program may use at most 64 MiB of HBM per device.

v0:
```python
import jax
import jax.numpy as jnp
from jax import lax
from jax.sharding import PartitionSpec as P

learn_rate = 0.1
hold_rate = 0.8


def in_blocks(array, dim, devices):
    shape = array.shape
    tiles = array.reshape(*shape[:dim], devices, shape[dim] // devices, *shape[dim + 1 :])
    return jnp.moveaxis(tiles, dim, 0)


def one_scatter(arrays, axis, dims):
    devices = lax.axis_size(axis)
    tiles = [in_blocks(a, dim, devices) for a, dim in zip(arrays, dims)]
    lines = jnp.concatenate([b.reshape(devices, -1) for b in tiles], axis=1)
    span = max(16, -(-lines.shape[1] // 1024) * 8)
    lines = jnp.pad(lines, ((0, 0), (0, span * 128 - lines.shape[1]))).reshape(-1, 128)
    line, at, finished = (lax.psum_scatter(lines, axis, tiled=True).reshape(-1), 0, [])
    for b in tiles:
        part = b[0]
        finished.append(line[at : at + part.size].reshape(part.shape))
        at += part.size
    return tuple(finished)


def sent_to_all(array, axis):
    copies = jnp.broadcast_to(array, (lax.axis_size(axis), *array.shape))
    return lax.all_to_all(copies, axis, split_axis=0, concat_axis=0, tiled=True)


def of_everyone(array, axis):
    return sent_to_all(array, axis).sum(axis=0)


def in_one(arrays, axis):
    line, at, finished = (jnp.concatenate([a.reshape(-1) for a in arrays]), 0, [])
    so_far = of_everyone(line, axis)
    for a in arrays:
        finished.append(so_far[at : at + a.size].reshape(a.shape))
        at += a.size
    return tuple(finished)


def gather_turned(arrays, axis, dims):
    turned = [jnp.moveaxis(a, dim, 0) for a, dim in zip(arrays, dims)]
    both = jnp.concatenate([t.reshape(len(t), -1) for t in turned], axis=1)
    filled, at, finished = (lax.all_gather(both, axis, axis=0, tiled=True), 0, [])
    for t, dim in zip(turned, dims):
        slab = filled[:, at : at + t[0].size].reshape(-1, *t.shape[1:])
        finished.append(jnp.moveaxis(slab, 0, dim))
        at += t[0].size
    return tuple(finished)


def on_device(
    partial_up,
    partial_down,
    partial_norm,
    partial_bias,
    master_up,
    master_down,
    master_norm,
    master_bias,
    memory_up,
    memory_down,
    memory_norm,
    memory_bias,
):
    mean_up, mean_down = tuple(
        (
            part.astype(jnp.float32)
            for part in one_scatter(
                (partial_up[0].astype(jnp.bfloat16), partial_down[0].astype(jnp.bfloat16)),
                "batch",
                (0, 1),
            )
        )
    )
    whole_norm, whole_bias = in_one((partial_norm[0], partial_bias[0]), "batch")
    place = lax.axis_index("batch")
    mean_norm = lax.dynamic_slice_in_dim(
        whole_norm, place * master_norm.shape[0], master_norm.shape[0]
    )
    mean_bias = lax.dynamic_slice_in_dim(
        whole_bias, place * master_bias.shape[0], master_bias.shape[0]
    )
    mean_rate = lax.axis_size("batch") ** (-0.5)
    mean_up = mean_up * mean_rate
    mean_down = mean_down * mean_rate
    mean_norm = mean_norm * mean_rate
    mean_bias = mean_bias * mean_rate
    state_new_up = hold_rate * memory_up + mean_up
    stepped_up = master_up - learn_rate * state_new_up
    state_new_down = hold_rate * memory_down + mean_down
    stepped_down = master_down - learn_rate * state_new_down
    state_new_norm = hold_rate * memory_norm + mean_norm
    stepped_norm = master_norm - learn_rate * state_new_norm
    state_new_bias = hold_rate * memory_bias + mean_bias
    stepped_bias = master_bias - learn_rate * state_new_bias
    compute_up, compute_down, compute_norm, compute_bias = gather_turned(
        (
            stepped_up.astype(jnp.bfloat16),
            stepped_down.astype(jnp.bfloat16),
            stepped_norm.astype(jnp.bfloat16),
            stepped_bias.astype(jnp.bfloat16),
        ),
        "batch",
        (0, 1, 0, 0),
    )
    return (
        compute_up,
        compute_down,
        compute_norm,
        compute_bias,
        stepped_up,
        stepped_down,
        stepped_norm,
        stepped_bias,
        state_new_up,
        state_new_down,
        state_new_norm,
        state_new_bias,
    )


def solution(mesh):
    return jax.shard_map(
        on_device,
        mesh=mesh,
        in_specs=(
            P(("shift", "batch"), None, "cols"),
            P(("shift", "batch"), "cols", None),
            P(("shift", "batch"), None),
            P(("shift", "batch"), None),
            P(("shift", "batch"), "cols"),
            P(("shift", "cols"), "batch"),
            P(("shift", "batch")),
            P(("shift", "batch")),
            P(("shift", "batch"), "cols"),
            P(("shift", "cols"), "batch"),
            P(("shift", "batch")),
            P(("shift", "batch")),
        ),
        out_specs=(
            P("shift", "cols"),
            P(("shift", "cols"), None),
            P("shift"),
            P("shift"),
            P(("shift", "batch"), "cols"),
            P(("shift", "cols"), "batch"),
            P(("shift", "batch")),
            P(("shift", "batch")),
            P(("shift", "batch"), "cols"),
            P(("shift", "cols"), "batch"),
            P(("shift", "batch")),
            P(("shift", "batch")),
        ),
        check_vma=False,
    )
```

profile of v0, /device:TPU:2, one launch (start us, length us, event | category | flops | bytes accessed | tf_op | source)
XLA Modules:
  0.0 193.8 jit_solution(17056441579653898916)
XLA Ops:
  7.2 0.0 copy-start
  7.2 0.0 reduce-scatter.2.cloned.1.call-start
  7.2 1.9 convert_element_type.34
  9.2 1.4 convert_element_type.35
  10.6 0.0 copy-done
  10.6 1.5 copy.50
  12.0 3.0 %copy.51 = bf16[16,768,48]{2,1,0:T(8,128)(2,1)S(1)} copy(bf16[16,768,48]{1,2,0:T(8,128)(2,1)} %bitcast.11) | data formatting | bytes 2359296 | tf_op jit(solution)/shard_map/transpose | solution.py:13
  15.0 7.1 %reshape.64 = bf16[16,36864]{1,0:T(8,128)(2,1)} reshape(bf16[16,768,48]{2,1,0:T(8,128)(2,1)S(1)} %copy.51) | data formatting | bytes 2359296 | tf_op jit(solution)/shard_map/reshape | solution.py:19
  22.2 1.8 pad_maximum_fusion
  23.9 2.1 %reshape.65 = bf16[9216,128]{1,0:T(8,128)(2,1)} reshape(bf16[16,73728]{1,0:T(8,128)(2,1)S(1)} %pad_maximum_fusion) | data formatting | bytes 4718592 | tf_op jit(solution)/shard_map/reshape | solution.py:21
  26.1 0.0 copy-start.5
  26.1 0.0 copy-start.6
  26.1 0.0 copy-start.7
  26.1 0.0 copy-start.8
  26.1 0.0 copy-start.9
  26.1 0.0 copy-start.10
  26.1 0.0 copy-start.1
  26.1 0.0 copy-start.2
  26.1 0.0 copy-start.3
  26.2 0.0 copy-start.4
  26.2 0.0 reduce-scatter.2.cloned.1.call-update
  26.2 0.6 copy-done.5
  26.8 0.0 copy-done.6
  26.8 0.7 broadcast_in_dim.3
  27.5 15.2 %all-to-all-start = ((f32[16,1,1536]{2,1,0:T(1,128)}), f32[16,1,1536]{2,1,0:T(1,128)S(1)}, u32[]{:S(2)}, u32[]{:S(2)}) async-start(f32[16,1,1536]{2,1,0:T(1,128)} %broadcast_in_dim.3), calls=%async_computation.1 | async-start | bytes 196608 | tf_op jit(solution)/shard_map/all_to_all | solution.py:32
  42.7 0.0 all-gather.2.cloned.1.call-start
  42.8 13.6 %all-to-all-done = f32[16,1,1536]{2,1,0:T(1,128)S(1)} async-done(((f32[16,1,1536]{2,1,0:T(1,128)}), f32[16,1,1536]{2,1,0:T(1,128)S(1)}, u32[]{:S(2)}, u32[]{:S(2)}) %all-to-all-start) | async-done | bytes 98336 | tf_op jit(solution)/shard_map/all_to_all | solution.py:32
  56.4 0.1 reduce_sum.9
  56.5 0.0 copy-done.7
  56.5 0.0 copy-done.8
  56.5 0.0 copy-done.9
  56.5 0.0 copy-done.10
  56.5 0.6 convert_bitcast_fusion.1
  57.1 0.1 copy.55
  57.2 0.1 copy.54
  57.3 48.8 %reduce-scatter.2.cloned.1.call-done = bf16[576,128]{1,0:T(8,128)(2,1)} async-done(((bf16[9216,128]{1,0:T(8,128)(2,1)}), bf16[576,128]{1,0:T(8,128)(2,1)}) %reduce-scatter.2.cloned.1.call-update) | async-done | bytes 147472 | tf_op jit(solution)/shard_map/reduce_scatter | solution.py:22
  106.1 0.9 convert_multiply_fusion
  107.1 0.2 mul.72
  107.3 0.1 copy.52
  107.4 0.0 copy-done.1
  107.4 0.0 copy-done.2
  107.4 0.7 fusion
  108.2 0.0 copy-done.3
  108.2 0.0 copy-done.4
  108.2 0.7 convert_bitcast_fusion
  108.9 0.8 concatenate.11
  109.7 0.0 all-gather.2.cloned.1.call-update
  109.7 71.1 %all-gather.2.cloned.1.call-done = bf16[768,1538]{1,0:T(8,128)(2,1)} async-done(((bf16[48,1538]{1,0:T(8,128)(2,1)}), bf16[768,1538]{1,0:T(8,128)(2,1)}) %all-gather.2.cloned.1.call-update) | async-done | bytes 2362384 | tf_op jit(solution)/shard_map/all_gather | solution.py:51
  180.8 2.8 %slice_bitcast_fusion = (bf16[768,768]{0,1:T(8,128)(2,1)S(1)}, bf16[768,768]{1,0:T(8,128)(2,1)}) fusion(bf16[768,1538]{1,0:T(8,128)(2,1)} %all-gather.2.cloned.1.call-done), kind=kLoop, calls=%fused_computation.1 | loop fusion | bytes 4718592 | tf_op jit(solution)/shard_map/transpose | solution.py:54
  183.6 1.4 copy.56
  185.0 1.9 slice_reduce_fusion
  (5 shorter events, 0.1 us)
Async XLA Ops:
  7.2 3.4 %copy-start = (f32[1,768,768]{2,1,0:T(8,128)S(1)}, f32[1,768,768]{2,1,0:T(8,128)}, u32[]{:S(2)}) copy-start(f32[1,768,768]{2,1,0:T(8,128)} %param.13) | copy-start | bytes 7077892
  7.2 98.9 %reduce-scatter.2.cloned.1.call-start = ((), (), s32[]{:S(2)}) async-start(), calls=%async_computation.2 | async-start | bytes 2506752 | tf_op jit(solution)/shard_map/reduce_scatter | solution.py:22
  26.1 0.7 copy-start.5
  26.1 0.7 copy-start.6
  26.1 30.4 %copy-start.7 = (f32[48]{0:T(128)S(1)}, f32[48]{0:T(128)}, u32[]{:S(2)}) copy-start(f32[48]{0:T(128)} %param.19) | copy-start | bytes 580
  26.1 30.4 %copy-start.8 = (f32[48]{0:T(128)S(1)}, f32[48]{0:T(128)}, u32[]{:S(2)}) copy-start(f32[48]{0:T(128)} %param.23) | copy-start | bytes 580
  26.1 30.4 %copy-start.9 = (f32[48]{0:T(128)S(1)}, f32[48]{0:T(128)}, u32[]{:S(2)}) copy-start(f32[48]{0:T(128)} %param.18) | copy-start | bytes 580
  26.1 30.4 %copy-start.10 = (f32[48]{0:T(128)S(1)}, f32[48]{0:T(128)}, u32[]{:S(2)}) copy-start(f32[48]{0:T(128)} %param.22) | copy-start | bytes 580
  26.1 81.3 %copy-start.1 = (f32[48,768]{1,0:T(8,128)S(1)}, f32[48,768]{1,0:T(8,128)}, u32[]{:S(2)}) copy-start(f32[48,768]{1,0:T(8,128)} %param.16) | copy-start | bytes 442372
  26.1 81.3 %copy-start.2 = (f32[48,768]{1,0:T(8,128)S(1)}, f32[48,768]{1,0:T(8,128)}, u32[]{:S(2)}) copy-start(f32[48,768]{1,0:T(8,128)} %param.20) | copy-start | bytes 442372
  26.1 82.0 %copy-start.3 = (f32[768,48]{0,1:T(8,128)S(1)}, f32[768,48]{0,1:T(8,128)}, u32[]{:S(2)}) copy-start(f32[768,48]{0,1:T(8,128)} %param.17) | copy-start | bytes 442372
  26.2 82.0 %copy-start.4 = (f32[768,48]{0,1:T(8,128)S(1)}, f32[768,48]{0,1:T(8,128)}, u32[]{:S(2)}) copy-start(f32[768,48]{0,1:T(8,128)} %param.21) | copy-start | bytes 442372
  27.5 28.9 %all-to-all-start = ((f32[16,1,1536]{2,1,0:T(1,128)}), f32[16,1,1536]{2,1,0:T(1,128)S(1)}, u32[]{:S(2)}, u32[]{:S(2)}) async-start(f32[16,1,1536]{2,1,0:T(1,128)} %broadcast_in_dim.3), calls=%async_computation.1 | async-start | bytes 196608 | tf_op jit(solution)/shard_map/all_to_all | solution.py:32
  42.7 138.1 %all-gather.2.cloned.1.call-start = ((), (), s32[]{:S(2)}) async-start(), calls=%async_computation.3 | async-start | bytes 2715648 | tf_op jit(solution)/shard_map/all_gather | solution.py:51
Sparse Core Ops, SparseCore 0:
  26.3 79.7 reduce-scatter.1
  109.8 70.9 all-gather.1
where the time goes:
time: 194 us
  waiting for transfers between devices  134 us (69%)
  local copies, waits for them, and re-layouts  23.9 us (12%)
  starting transfers between devices  15.3 us (8%)
  between operations  14.2 us (7%)
  other arithmetic  6.85 us (4%)
    all_gather x1, waiting for transfers between devices, gather_turned(): lax.all_gather(both, axis, axis=0, tiled=True)  71.1 us
    reduce_scatter x1, waiting for transfers between devices, one_scatter(): lax.psum_scatter(lines, axis, tiled=True).reshape(-1)  48.8 us
    all_to_all x1, starting transfers between devices, sent_to_all(): return lax.all_to_all(copies, axis, split_axis=0, concat_axis=0, tiled=True)  15.2 us
    all_to_all x1, waiting for transfers between devices, sent_to_all(): return lax.all_to_all(copies, axis, split_axis=0, concat_axis=0, tiled=True)  13.6 us
    reshape x1, local copies, waits for them, and re-layouts, one_scatter(): lines = jnp.concatenate([b.reshape(devices, -1) for b in tiles], axis=1)  7.14 us
  transfers between devices with their start and end apart: 3, of which 3 were waited for; matrix products, arithmetic and copies ran while one was open for 1% of the time, Pallas kernels for 0%

commit v1 on v0

--- a/solution.py
+++ b/solution.py
@@ -48,7 +48,13 @@
 def gather_turned(arrays, axis, dims):
     turned = [jnp.moveaxis(a, dim, 0) for a, dim in zip(arrays, dims)]
     both = jnp.concatenate([t.reshape(len(t), -1) for t in turned], axis=1)
-    filled, at, finished = (lax.all_gather(both, axis, axis=0, tiled=True), 0, [])
+    filled, at, finished = (
+        jnp.concatenate(
+            lax.all_to_all(jnp.stack([both] * lax.axis_size(axis)), axis, 0, 0), axis=0
+        ),
+        0,
+        [],
+    )
     for t, dim in zip(turned, dims):
         slab = filled[:, at : at + t[0].size].reshape(-1, *t.shape[1:])
         finished.append(jnp.moveaxis(slab, 0, dim))

time: 194 us -> 235 us (1.21)
  the two profiles are of different devices: /device:TPU:2 before, /device:TPU:46 now
where the time goes in v1:
time: 235 us; the launch traced here: 234 us
  blocking collectives  116 us (49%)
  waiting for transfers between devices  61 us (26%)
  local copies, waits for them, and re-layouts  20.7 us (9%)
  starting transfers between devices  15.2 us (6%)
  between operations  14.2 us (6%)
  other arithmetic  6.85 us (3%)
    all_to_all x1, blocking collectives, gather_turned(): lax.all_to_all(jnp.stack([both] * lax.axis_size(axis)), axis, 0, 0)  116 us
    reduce_scatter x1, waiting for transfers between devices, one_scatter(): lax.psum_scatter(lines, axis, tiled=True).reshape(-1)  48 us
    all_to_all x1, starting transfers between devices, sent_to_all(): return lax.all_to_all(copies, axis, split_axis=0, concat_axis=0, tiled=True)  15.2 us
    all_to_all x1, waiting for transfers between devices, sent_to_all(): return lax.all_to_all(copies, axis, split_axis=0, concat_axis=0, tiled=True)  13 us
    reshape x1, local copies, waits for them, and re-layouts, one_scatter(): lines = jnp.concatenate([b.reshape(devices, -1) for b in tiles], axis=1)  7.14 us
  transfers between devices with their start and end apart: 2, of which 2 were waited for; matrix products, arithmetic and copies ran while one was open for 1% of the time, Pallas kernels for 0%

profile of v1, /device:TPU:46, one launch (start us, length us, event | category | flops | bytes accessed | tf_op | source)
XLA Modules:
  0.0 234.3 jit_solution(6543196915028198705)
XLA Ops:
  7.2 0.0 copy-start
  7.2 0.0 reduce-scatter.2.cloned.1.call-start
  7.2 1.9 convert_element_type.34
  9.2 1.4 convert_element_type.35
  10.6 0.0 copy-done
  10.6 1.5 copy.52
  12.0 3.0 %copy.53 = bf16[16,768,48]{2,1,0:T(8,128)(2,1)S(1)} copy(bf16[16,768,48]{1,2,0:T(8,128)(2,1)} %bitcast.14) | data formatting | bytes 2359296 | tf_op jit(solution)/shard_map/transpose | solution.py:13
  15.0 7.1 %reshape.69 = bf16[16,36864]{1,0:T(8,128)(2,1)} reshape(bf16[16,768,48]{2,1,0:T(8,128)(2,1)S(1)} %copy.53) | data formatting | bytes 2359296 | tf_op jit(solution)/shard_map/reshape | solution.py:19
  22.2 1.8 pad_maximum_fusion
  23.9 2.1 reshape.70
  26.1 0.0 copy-start.5
  26.1 0.0 copy-start.6
  26.1 0.0 copy-start.7
  26.1 0.0 copy-start.8
  26.1 0.0 copy-start.9
  26.1 0.0 copy-start.10
  26.1 0.0 copy-start.1
  26.1 0.0 copy-start.2
  26.1 0.0 copy-start.3
  26.1 0.0 copy-start.4
  26.2 0.0 reduce-scatter.2.cloned.1.call-update
  26.2 0.6 copy-done.5
  26.8 0.0 copy-done.6
  26.8 0.7 broadcast_in_dim.3
  27.5 15.2 %all-to-all-start = ((f32[16,1,1536]{2,1,0:T(1,128)}), f32[16,1,1536]{2,1,0:T(1,128)S(1)}, u32[]{:S(2)}, u32[]{:S(2)}) async-start(f32[16,1,1536]{2,1,0:T(1,128)} %broadcast_in_dim.3), calls=%async_computation.1 | async-start | bytes 196608 | tf_op jit(solution)/shard_map/all_to_all | solution.py:32
  42.7 13.0 %all-to-all-done = f32[16,1,1536]{2,1,0:T(1,128)S(1)} async-done(((f32[16,1,1536]{2,1,0:T(1,128)}), f32[16,1,1536]{2,1,0:T(1,128)S(1)}, u32[]{:S(2)}, u32[]{:S(2)}) %all-to-all-start) | async-done | bytes 98336 | tf_op jit(solution)/shard_map/all_to_all | solution.py:32
  55.8 0.1 reduce_sum.9
  55.8 0.0 copy-done.7
  55.9 0.0 copy-done.8
  55.9 0.0 copy-done.9
  55.9 0.0 copy-done.10
  55.9 0.6 convert_bitcast_fusion.1
  56.5 0.1 copy.57
  56.6 0.1 copy.56
  56.7 48.0 %reduce-scatter.2.cloned.1.call-done = bf16[576,128]{1,0:T(8,128)(2,1)} async-done(((bf16[9216,128]{1,0:T(8,128)(2,1)}), bf16[576,128]{1,0:T(8,128)(2,1)}) %reduce-scatter.2.cloned.1.call-update) | async-done | bytes 147472 | tf_op jit(solution)/shard_map/reduce_scatter | solution.py:22
  104.7 0.9 convert_multiply_fusion
  105.7 0.2 mul.72
  105.8 0.1 copy.54
  106.0 0.0 copy-done.1
  106.0 0.0 copy-done.2
  106.0 0.7 fusion
  106.7 0.0 copy-done.3
  106.7 0.0 copy-done.4
  106.7 0.7 convert_bitcast_fusion
  107.5 0.1 concatenate.11
  107.6 0.2 stack.2
  107.8 116.2 %all_to_all.11 = bf16[16,48,1538]{2,1,0:T(8,128)(2,1)S(1)} all-to-all(bf16[16,48,1538]{2,1,0:T(8,128)(2,1)S(1)} %stack.2), channel_id=1, replica_groups=mesh['shift'=8,'batch'=16,'cols'=4] {'batch'}, dimensions={0} | all-to-all | bytes 4724736 | tf_op jit(solution)/shard_map/all_to_all | solution.py:53
  224.0 0.9 slice_reduce_fusion
  224.9 1.2 slice_bitcast_fusion
  226.0 1.4 copy.58
  (5 shorter events, 0.1 us)
Async XLA Ops:
  7.2 3.4 %copy-start = (f32[1,768,768]{2,1,0:T(8,128)S(1)}, f32[1,768,768]{2,1,0:T(8,128)}, u32[]{:S(2)}) copy-start(f32[1,768,768]{2,1,0:T(8,128)} %param.13) | copy-start | bytes 7077892
  7.2 97.5 %reduce-scatter.2.cloned.1.call-start = ((), (), s32[]{:S(2)}) async-start(), calls=%async_computation.3 | async-start | bytes 2506752 | tf_op jit(solution)/shard_map/reduce_scatter | solution.py:22
  26.1 0.7 copy-start.5
  26.1 0.7 copy-start.6
  26.1 29.8 %copy-start.7 = (f32[48]{0:T(128)S(1)}, f32[48]{0:T(128)}, u32[]{:S(2)}) copy-start(f32[48]{0:T(128)} %param.19) | copy-start | bytes 580
  26.1 29.8 %copy-start.8 = (f32[48]{0:T(128)S(1)}, f32[48]{0:T(128)}, u32[]{:S(2)}) copy-start(f32[48]{0:T(128)} %param.23) | copy-start | bytes 580
  26.1 29.8 %copy-start.9 = (f32[48]{0:T(128)S(1)}, f32[48]{0:T(128)}, u32[]{:S(2)}) copy-start(f32[48]{0:T(128)} %param.18) | copy-start | bytes 580
  26.1 29.8 %copy-start.10 = (f32[48]{0:T(128)S(1)}, f32[48]{0:T(128)}, u32[]{:S(2)}) copy-start(f32[48]{0:T(128)} %param.22) | copy-start | bytes 580
  26.1 79.9 %copy-start.1 = (f32[48,768]{1,0:T(8,128)S(1)}, f32[48,768]{1,0:T(8,128)}, u32[]{:S(2)}) copy-start(f32[48,768]{1,0:T(8,128)} %param.16) | copy-start | bytes 442372
  26.1 79.9 %copy-start.2 = (f32[48,768]{1,0:T(8,128)S(1)}, f32[48,768]{1,0:T(8,128)}, u32[]{:S(2)}) copy-start(f32[48,768]{1,0:T(8,128)} %param.20) | copy-start | bytes 442372
  26.1 80.6 %copy-start.3 = (f32[768,48]{0,1:T(8,128)S(1)}, f32[768,48]{0,1:T(8,128)}, u32[]{:S(2)}) copy-start(f32[768,48]{0,1:T(8,128)} %param.17) | copy-start | bytes 442372
  26.1 80.6 %copy-start.4 = (f32[768,48]{0,1:T(8,128)S(1)}, f32[768,48]{0,1:T(8,128)}, u32[]{:S(2)}) copy-start(f32[768,48]{0,1:T(8,128)} %param.21) | copy-start | bytes 442372
  27.5 28.3 %all-to-all-start = ((f32[16,1,1536]{2,1,0:T(1,128)}), f32[16,1,1536]{2,1,0:T(1,128)S(1)}, u32[]{:S(2)}, u32[]{:S(2)}) async-start(f32[16,1,1536]{2,1,0:T(1,128)} %broadcast_in_dim.3), calls=%async_computation.1 | async-start | bytes 196608 | tf_op jit(solution)/shard_map/all_to_all | solution.py:32
Sparse Core Ops, SparseCore 0:
  26.3 78.3 reduce-scatter.1
